TPU v7x, 32 devices: a whole 2x2x4 slice. The times are simulated.
32 devices in a mesh: member: 4 (over y, x), lat: 2 (over core), lon: 4 (over z).
Axes of the slice: x: 2, y: 2, z: 4, core: 2. Of those that a mesh axis runs over, the one named last changes fastest.
Arguments:
- ice_flux: float32 [8, 64, 8, 512], P(('member', 'lat'), 'lon'), parts along dimension 0, may hold values from 0.5 to 1.5
- ice_frac: float32 [8, 64, 512], P(('member', 'lat'), 'lon'), parts along dimension 0, may hold values from 0.05 to 1
- ice_mask: int32 [8, 64, 512], P(('member', 'lat'), 'lon'), parts along dimension 0, may hold values 0 or 1
- ice_area: float32 [8, 64, 512], P(('member', 'lat'), 'lon'), parts along dimension 0, may hold values from 0.7 to 44.3
- route: int32 [8, 64], P(('member', 'lat'), 'lon'), parts along dimension 0, may hold values from 0 to 63, as said below
- ocean_area: float32 [512, 512], P(('member', 'lat'), 'lon'), parts along dimension 0, may hold values from 0.7 to 44.3
- ocean_wet: int32 [512, 512], P(('member', 'lat'), 'lon'), parts along dimension 0, may hold values 0 or 1
- exponent: int32 [8], replicated, may hold values from 0 to 3
Outputs:
- ocean_flux: float32 [8, 512, 512], P(None, ('member', 'lat'), 'lon'), parts along dimension 1
- source_total: float32 [32], P('member'), parts along dimension 0
There are 4 independent parts, one for each index of `member`. A program takes and returns all parts, laid end to end along the dimension named above; an argument that names none is the same for every part. Nothing has to cross between parts.
Inputs may be any that keep to these rules, and one draw needn't show every extreme that they name: Within each latitude tile row, route is a permutation of 0 to 63. The 16 entries of one device name, for every longitude tile k that they name (route // 16 == k), exactly 4 blocks of it.
All inputs are finite; a program needn't handle non-finite values. No bound on the sum of `ice_mask` or of `ocean_wet` on one device may be relied on, other than what follows from the above.
Results may differ from a plain program's by a relative error of at most 0.0003.
Values sent between devices are 32-bit elements; how exact they have to be, the bound alone decides.
A program may use at most 64 MiB of HBM per device.

v0:
```python
import jax
import jax.numpy as jnp
from jax import lax
from jax.sharding import PartitionSpec as P

quantum = 1024.0
limb_base = 65536


def local_units(values, axes):
    return jnp.sum((values * quantum).astype(jnp.int32), axis=axes)


def split_units(total):
    upper_part = total // limb_base
    return (upper_part, total - upper_part * limb_base)


def join_units(upper_part, lower_part):
    return (upper_part.astype(jnp.float32) * limb_base + lower_part.astype(jnp.float32)) / quantum


def body(ice_flux, ice_frac, ice_mask, ice_area, route, ocean_area, ocean_wet, exponent):
    block_count = route.shape[1]
    field_count = ice_flux.shape[2]
    block_cells = ice_flux.shape[3]
    width_cells = ocean_area.shape[1]
    band_rows = block_cells // width_cells
    tile_count = lax.axis_size("lon")
    amount = ice_area * ice_frac * ice_mask.astype(jnp.float32)
    carried = ice_flux * amount[:, :, None, :]
    source_upper, source_lower = split_units(local_units(carried, (0, 1, 3)))
    block_ids = jnp.arange(block_count, dtype=jnp.int32)
    capacity = max(2, block_count // tile_count)
    targets = route[0]
    target_tile = targets // block_count
    block_row = targets % block_count
    earlier = (target_tile[:, None] == target_tile[None, :]) & (
        block_ids[:, None] > block_ids[None, :]
    )
    ordinal = jnp.sum(earlier.astype(jnp.int32), axis=1)
    slot_index = target_tile * capacity + ordinal
    slot_ids = jnp.arange(tile_count * capacity, dtype=jnp.int32)
    selector = (slot_index[None, :] == slot_ids[:, None]).astype(jnp.float32)
    outgoing = jnp.einsum("qs,sfc->qfc", selector, carried[0], precision=lax.Precision.HIGHEST)
    outgoing_rows = (
        jnp.dot(selector, (block_row + 1).astype(jnp.float32), precision=lax.Precision.HIGHEST)
        - 1.0
    )
    received_rows, arrived_rows = (
        lax.all_to_all(outgoing, "lon", split_axis=0, concat_axis=0, tiled=True),
        lax.all_to_all(outgoing_rows, "lon", split_axis=0, concat_axis=0, tiled=True),
    )
    position_mapper = (arrived_rows[None, :] == block_ids.astype(jnp.float32)[:, None]).astype(
        jnp.float32
    )
    block_groups = jnp.einsum(
        "nw,whl->nhl", position_mapper, received_rows, precision=lax.Precision.HIGHEST
    )
    mapped = block_groups.reshape(block_count, field_count, band_rows, width_cells).transpose(
        1, 0, 2, 3
    )
    mapped = mapped.reshape(field_count, block_count * band_rows, width_cells)
    wet_cover = ocean_wet.astype(jnp.float32)
    target_upper, target_lower = split_units(local_units(wet_cover * mapped, (1, 2)))
    wet_upper, wet_lower = split_units(local_units(ocean_area * wet_cover, (0, 1)))
    source_upper, source_lower, target_upper, target_lower, wet_upper, wet_lower = lax.psum(
        (source_upper, source_lower, target_upper, target_lower, wet_upper, wet_lower),
        ("lat", "lon"),
    )
    source = join_units(source_upper, source_lower)
    target = join_units(target_upper, target_lower)
    wet_area = join_units(wet_upper, wet_lower)
    correction = (source - target) / wet_area
    scaling = jnp.left_shift(jnp.ones_like(exponent), exponent).astype(jnp.float32)
    ocean_flux = (
        wet_cover * scaling[:, None, None] * (mapped / ocean_area + correction[:, None, None])
    )
    return (ocean_flux, source * scaling)


def solution(mesh):
    placed = (
        P(("member", "lat"), "lon", None, None),
        P(("member", "lat"), "lon", None),
        P(("member", "lat"), "lon", None),
        P(("member", "lat"), "lon", None),
        P(("member", "lat"), "lon"),
        P(("member", "lat"), "lon"),
        P(("member", "lat"), "lon"),
        P(),
    )
    return jax.shard_map(
        body,
        mesh=mesh,
        in_specs=placed,
        out_specs=(P(None, ("member", "lat"), "lon"), P("member")),
        check_vma=False,
    )
```

profile of v0, /device:TPU:0, one launch (start us, length us, event | category | flops | bytes accessed | tf_op | source)
XLA Modules:
  0.0 37.0 jit_solution(16438708426224895348)
XLA Ops:
  0.6 0.0 copy-start.5
  0.6 0.0 copy-start.3
  0.6 0.7 %fusion.29 = s32[16]{0:T(128)S(1)} fusion(s32[1,16]{1,0:T(1,128)} %param.12), kind=kLoop, calls=%fused_computation.62 | loop fusion | flops 240 | bytes 128 | tf_op jit(solution)/shard_map/eq | solution.py:38
  1.4 0.0 copy-done.5
  1.4 0.2 convert_reduce_fusion.2
  1.6 0.1 fusion
  1.7 0.7 %all_to_all.9 = f32[4,4,1]{1,0,2:T(4,128)} reshape(f32[16]{0:T(128)S(1)} %fusion) | data formatting | bytes 128 | tf_op jit(solution)/shard_map/all_to_all | solution.py:52
  2.4 6.3 %all-to-all-start = ((f32[4,4,1]{1,2,0:T(1,128)}), f32[4,4,1]{1,2,0:T(1,128)S(1)}, u32[]{:S(2)}, u32[]{:S(2)}) async-start(f32[4,4,1]{1,2,0:T(1,128)} %bitcast.6), calls=%async_computation | async-start | bytes 4096 | tf_op jit(solution)/shard_map/all_to_all | solution.py:52
  8.8 0.8 %multiply_bitcast_fusion.1 = f32[16,512]{1,0:T(8,128)S(1)} fusion(s32[1,16,512]{2,1,0:T(8,128)S(1)} %copy-done.3, f32[1,16,512]{2,1,0:T(8,128)} %param.11, f32[1,16,512]{2,1,0:T(8,128)} %param.9), kind=kLoop, calls=%fused_computation.14 | loop fusion | flops 24576 | bytes 131072 | tf_op jit(solution)/shard_map/mul | solution.py:31
  9.5 1.0 %multiply_bitcast_fusion = f32[16,8,512]{2,1,0:T(8,128)S(1)} fusion(f32[1,16,8,512]{3,2,1,0:T(8,128)} %param.8, f32[16,512]{1,0:T(8,128)S(1)} %multiply_bitcast_fusion.1), kind=kLoop, calls=%fused_computation.12 | loop fusion | flops 65536 | bytes 557056 | tf_op jit(solution)/shard_map/squeeze | solution.py:45
  10.5 0.0 copy-start.4
  10.5 0.0 copy-start.1
  10.6 0.0 copy-start.2
  10.6 0.4 %fusion.6 = f32[16,8,512]{2,0,1:T(8,128)S(1)} fusion(f32[16,8,512]{2,1,0:T(8,128)S(1)} %multiply_bitcast_fusion, s32[16]{0:T(128)S(1)} %fusion.21), kind=kOutput, calls=%fused_computation.8 | convolution fusion | flops 12583168 | bytes 524352 | tf_op jit(solution)/shard_map/qs,sfc->qfc/dot_general | solution.py:45
  11.0 0.2 copy-done.4
  11.2 0.1 copy-done.1
  11.3 0.0 copy-done.2
  11.3 0.6 %convert_reduce_fusion.1 = (s32[]{:T(128)}, f32[64,128]{1,0:T(8,128)S(1)}) fusion(f32[64,128]{1,0:T(8,128)S(1)} %copy-done.1, s32[64,128]{1,0:T(8,128)S(1)} %copy-done.2), kind=kLoop, calls=%fused_computation.13 | loop fusion | flops 40959 | bytes 98308 | tf_op jit(solution)/shard_map/reduce_sum | solution.py:11
  12.0 0.9 %copy.14 = f32[16,8,512]{2,1,0:T(8,128)} copy(f32[16,8,512]{2,0,1:T(8,128)S(1)} %fusion.6) | data formatting | bytes 524288 | tf_op jit(solution)/shard_map/qs,sfc->qfc/dot_general | solution.py:45
  12.8 1.4 %all-to-all-done = f32[4,4,1]{1,2,0:T(1,128)S(1)} async-done(((f32[4,4,1]{1,2,0:T(1,128)}), f32[4,4,1]{1,2,0:T(1,128)S(1)}, u32[]{:S(2)}, u32[]{:S(2)}) %all-to-all-start) | async-done | bytes 96 | tf_op jit(solution)/shard_map/all_to_all | solution.py:52
  14.2 3.9 %all-to-all-start.1 = ((f32[16,8,512]{2,1,0:T(8,128)}), f32[16,8,512]{2,1,0:T(8,128)S(1)}, u32[]{:S(2)}, u32[]{:S(2)}) async-start(f32[16,8,512]{2,1,0:T(8,128)} %copy.14), calls=%async_computation.1 | async-start | bytes 524288 | tf_op jit(solution)/shard_map/all_to_all | solution.py:51
  21.3 0.2 convert_reduce_fusion
  21.5 0.5 %broadcast.161 = f32[]{:T(128)} broadcast(f32[]{:T(128)} %constant.126), dimensions={} | broadcast | bytes 8 | tf_op jit(solution)/shard_map/all_to_all | solution.py:52
  22.0 0.7 %reduce.4 = f32[4,4]{1,0:T(4,128)S(1)} reduce(f32[4,4,1]{1,2,0:T(1,128)S(1)} %all-to-all-done, f32[]{:T(128)} %broadcast.161), dimensions={2}, to_apply=%all_to_all.10.reduce_sub_computation.3 | reduce | bytes 132 | tf_op jit(solution)/shard_map/all_to_all | solution.py:52
  22.7 0.1 eq.52
  22.8 3.6 %all-to-all-done.1 = f32[16,8,512]{2,1,0:T(8,128)S(1)} async-done(((f32[16,8,512]{2,1,0:T(8,128)}), f32[16,8,512]{2,1,0:T(8,128)S(1)}, u32[]{:S(2)}, u32[]{:S(2)}) %all-to-all-start.1) | async-done | bytes 262176 | tf_op jit(solution)/shard_map/all_to_all | solution.py:51
  26.4 0.4 %fusion.4 = f32[16,8,512]{2,0,1:T(8,128)S(1)} fusion(f32[16,8,512]{2,1,0:T(8,128)S(1)} %all-to-all-done.1, f32[16]{0:T(128)S(1)} %eq.52, f32[16]{0:T(128)S(1)} %iota_convert_fusion), kind=kOutput, calls=%fused_computation.6 | convolution fusion | flops 12583168 | bytes 524416 | tf_op jit(solution)/shard_map/nw,whl->nhl/dot_general | solution.py:57
  26.8 0.1 reshape.55
  26.9 0.3 fusion.3
  27.2 7.2 %all-reduce = (s32[8]{0:T(128)S(1)}, s32[8]{0:T(128)S(1)}, s32[]{:T(128)}, s32[]{:T(128)}, s32[8]{0:T(128)S(1)}, /*index=5*/s32[8]{0:T(128)S(1)}) all-reduce(s32[8]{0:T(128)S(1)} %get-tuple-element.10, s32[8]{0:T(128)S(1)} %get-tuple-element.11, s32[]{:T(128)S(6)} %select_n.37, ...), channel_id=1, replica_groups=mesh['member'=4,'lat'=2,'lon'=4] {'lat','lon'}, use_global_device_ids=true, to_apply=%region_6.7 | all-reduce | flops 34 | bytes 272 | tf_op jit(solution)/shard_map/psum | solution.py:67
  35.7 0.5 %fusion.28 = (f32[8]{0:T(128)}, f32[8]{0:T(128)S(1)}) fusion(s32[8]{0:T(128)S(1)} %copy-done.4, s32[8]{0:T(128)S(1)} %get-tuple-element.6, s32[8]{0:T(128)S(1)} %get-tuple-element.7, f32[]{:T(128)S(6)} %div.93, s32[8]{0:T(128)S(1)} %get-tuple-element.2, s32[8]{0:T(128)S(1)} %get-tuple-element.3), kind=kLoop, calls=%fused_computation.61 | loop fusion | flops 120 | bytes 228 | tf_op jit(solution)/shard_map/mul | solution.py:79
  36.2 0.8 %add_multiply_fusion = f32[8,64,128]{2,1,0:T(8,128)} fusion(f32[8,64,128]{2,1,0:T(8,128)S(1)} %bitcast.56, f32[8]{0:T(128)S(1)} %get-tuple-element.15, f32[64,128]{1,0:T(8,128)S(1)} %copy-done.1, f32[8]{0:T(128)S(1)} %shift-left_convert_fusion, f32[64,128]{1,0:T(8,128)S(1)} %get-tuple-element.13), kind=kLoop, calls=%fused_computation.10 | loop fusion | flops 262144 | bytes 589888 | tf_op jit(solution)/shard_map/mul | solution.py:77
  (9 shorter events, 0.1 us)
Async XLA Ops:
  0.6 0.7 %copy-start.5 = (s32[1,16]{1,0:T(1,128)S(1)}, s32[1,16]{1,0:T(1,128)}, u32[]{:S(2)}) copy-start(s32[1,16]{1,0:T(1,128)} %param.12) | copy-start | bytes 196
  0.6 8.1 %copy-start.3 = (s32[1,16,512]{2,1,0:T(8,128)S(1)}, s32[1,16,512]{2,1,0:T(8,128)}, u32[]{:S(2)}) copy-start(s32[1,16,512]{2,1,0:T(8,128)} %param.10) | copy-start | bytes 98308
  2.4 11.8 %all-to-all-start = ((f32[4,4,1]{1,2,0:T(1,128)}), f32[4,4,1]{1,2,0:T(1,128)S(1)}, u32[]{:S(2)}, u32[]{:S(2)}) async-start(f32[4,4,1]{1,2,0:T(1,128)} %bitcast.6), calls=%async_computation | async-start | bytes 4096 | tf_op jit(solution)/shard_map/all_to_all | solution.py:52
  10.5 0.7 %copy-start.4 = (s32[8]{0:T(128)S(1)}, s32[8]{0:T(128)}, u32[]{:S(2)}) copy-start(s32[8]{0:T(128)} %param.15) | copy-start | bytes 100
  10.5 0.8 %copy-start.1 = (f32[64,128]{1,0:T(8,128)S(1)}, f32[64,128]{1,0:T(8,128)}, u32[]{:S(2)}) copy-start(f32[64,128]{1,0:T(8,128)} %param.13) | copy-start | bytes 98308
  10.6 0.8 %copy-start.2 = (s32[64,128]{1,0:T(8,128)S(1)}, s32[64,128]{1,0:T(8,128)}, u32[]{:S(2)}) copy-start(s32[64,128]{1,0:T(8,128)} %param.14) | copy-start | bytes 98308
  12.8 8.5 %copy-start = (f32[1,16,8,512]{3,2,1,0:T(8,128)S(1)}, f32[1,16,8,512]{3,2,1,0:T(8,128)}, u32[]{:S(2)}) copy-start(f32[1,16,8,512]{3,2,1,0:T(8,128)} %param.8) | copy-start | bytes 786436
  14.2 12.2 %all-to-all-start.1 = ((f32[16,8,512]{2,1,0:T(8,128)}), f32[16,8,512]{2,1,0:T(8,128)S(1)}, u32[]{:S(2)}, u32[]{:S(2)}) async-start(f32[16,8,512]{2,1,0:T(8,128)} %copy.14), calls=%async_computation.1 | async-start | bytes 524288 | tf_op jit(solution)/shard_map/all_to_all | solution.py:51
where the time goes:
time: 37.6 us; the launch traced here: 37 us
  starting transfers between devices  10.2 us (27%)
  blocking collectives  7.23 us (19%)
  other arithmetic  5.81 us (15%)
  between operations  5.28 us (14%)
  waiting for transfers between devices  4.93 us (13%)
  local copies, waits for them, and re-layouts  2.61 us (7%)
  matrix products  0.94 us (2%)
    psum x1, blocking collectives, body(): lax.psum((source_upper, source_lower, target_upper, target_lower, wet_upp...  7.23 us
    all_to_all x1, starting transfers between devices, body(): lax.all_to_all(outgoing_rows, 'lon', split_axis=0, concat_axis=0, tiled=T...  6.35 us
    all_to_all x1, starting transfers between devices, body(): lax.all_to_all(outgoing, 'lon', split_axis=0, concat_axis=0, tiled=True)  3.88 us
    all_to_all x1, waiting for transfers between devices, body(): lax.all_to_all(outgoing, 'lon', split_axis=0, concat_axis=0, tiled=True)  3.58 us
    all_to_all x1, waiting for transfers between devices, body(): lax.all_to_all(outgoing_rows, 'lon', split_axis=0, concat_axis=0, tiled=T...  1.35 us
    all_to_all x2, local copies, waits for them, and re-layouts, body(): lax.all_to_all(outgoing_rows, 'lon', split_axis=0, concat_axis=0, tiled=T...  1.21 us
    reduce_sum x3, other arithmetic, local_units(): return jnp.sum((values * quantum).astype(jnp.int32), axis=axes)  1.1 us
    squeeze x1, other arithmetic, body(): carried[0]  0.98 us
  transfers between devices with their start and end apart: 2, of which 2 were waited for; matrix products, arithmetic and copies ran while one was open for 14% of the time, Pallas kernels for 0%

commit v1 on v0

--- a/solution.py
+++ b/solution.py
@@ -65,8 +65,10 @@
     target_upper, target_lower = split_units(local_units(wet_cover * mapped, (1, 2)))
     wet_upper, wet_lower = split_units(local_units(ocean_area * wet_cover, (0, 1)))
     source_upper, source_lower, target_upper, target_lower, wet_upper, wet_lower = lax.psum(
-        (source_upper, source_lower, target_upper, target_lower, wet_upper, wet_lower),
-        ("lat", "lon"),
+        lax.psum(
+            (source_upper, source_lower, target_upper, target_lower, wet_upper, wet_lower), "lon"
+        ),
+        "lat",
     )
     source = join_units(source_upper, source_lower)
     target = join_units(target_upper, target_lower)

time: 37.6 us -> 39.2 us (1.043)
  blocking collectives: 7.23 us -> 8.87 us
    psum x0 -> x1, blocking collectives: none -> 2.46 us  [body(): lax.psum(lax.psum((source_upper, source_lower, target_upper, target_lower...]
    psum x1, blocking collectives: 7.23 us -> 6.42 us  [body(): lax.psum((source_upper, source_lower, target_upper, target_lower, wet_upp...]
  transfers between devices with their start and end apart: 2 -> 2, of which waited for: 2 -> 2; matrix products, arithmetic and copies ran while one was open for 14% -> 13% of each run, Pallas kernels for 0% -> 0%
where the time goes in v1:
time: 39.2 us; the launch traced here: 38.7 us
  starting transfers between devices  10.2 us (26%)
  blocking collectives  8.87 us (23%)
  other arithmetic  5.81 us (15%)
  between operations  5.28 us (13%)
  waiting for transfers between devices  4.93 us (13%)
  local copies, waits for them, and re-layouts  2.61 us (7%)
  matrix products  0.94 us (2%)
    psum x1, blocking collectives, body(): lax.psum((source_upper, source_lower, target_upper, target_lower, wet_upp...  6.42 us
    all_to_all x1, starting transfers between devices, body(): lax.all_to_all(outgoing_rows, 'lon', split_axis=0, concat_axis=0, tiled=T...  6.35 us
    all_to_all x1, starting transfers between devices, body(): lax.all_to_all(outgoing, 'lon', split_axis=0, concat_axis=0, tiled=True)  3.88 us
    all_to_all x1, waiting for transfers between devices, body(): lax.all_to_all(outgoing, 'lon', split_axis=0, concat_axis=0, tiled=True)  3.58 us
    psum x1, blocking collectives, body(): lax.psum(lax.psum((source_upper, source_lower, target_upper, target_lower...  2.46 us
    all_to_all x1, waiting for transfers between devices, body(): lax.all_to_all(outgoing_rows, 'lon', split_axis=0, concat_axis=0, tiled=T...  1.35 us
    all_to_all x2, local copies, waits for them, and re-layouts, body(): lax.all_to_all(outgoing_rows, 'lon', split_axis=0, concat_axis=0, tiled=T...  1.21 us
    reduce_sum x3, other arithmetic, local_units(): return jnp.sum((values * quantum).astype(jnp.int32), axis=axes)  1.1 us
  transfers between devices with their start and end apart: 2, of which 2 were waited for; matrix products, arithmetic and copies ran while one was open for 13% of the time, Pallas kernels for 0%

profile of v1, /device:TPU:0, one launch (start us, length us, event | category | flops | bytes accessed | tf_op | source)
XLA Modules:
  0.0 38.7 jit_solution(15088510409496898125)
XLA Ops:
  0.6 0.0 copy-start.5
  0.6 0.0 copy-start.3
  0.6 0.7 %fusion.29 = s32[16]{0:T(128)S(1)} fusion(s32[1,16]{1,0:T(1,128)} %param.12), kind=kLoop, calls=%fused_computation.62 | loop fusion | flops 240 | bytes 128 | tf_op jit(solution)/shard_map/eq | solution.py:38
  1.4 0.2 convert_reduce_fusion.2
  1.6 0.1 fusion
  1.7 0.7 %all_to_all.9 = f32[4,4,1]{1,0,2:T(4,128)} reshape(f32[16]{0:T(128)S(1)} %fusion) | data formatting | bytes 128 | tf_op jit(solution)/shard_map/all_to_all | solution.py:52
  2.4 6.3 %all-to-all-start = ((f32[4,4,1]{1,2,0:T(1,128)}), f32[4,4,1]{1,2,0:T(1,128)S(1)}, u32[]{:S(2)}, u32[]{:S(2)}) async-start(f32[4,4,1]{1,2,0:T(1,128)} %bitcast.6), calls=%async_computation | async-start | bytes 4096 | tf_op jit(solution)/shard_map/all_to_all | solution.py:52
  8.8 0.8 %multiply_bitcast_fusion.1 = f32[16,512]{1,0:T(8,128)S(1)} fusion(s32[1,16,512]{2,1,0:T(8,128)S(1)} %copy-done.3, f32[1,16,512]{2,1,0:T(8,128)} %param.11, f32[1,16,512]{2,1,0:T(8,128)} %param.9), kind=kLoop, calls=%fused_computation.14 | loop fusion | flops 24576 | bytes 131072 | tf_op jit(solution)/shard_map/mul | solution.py:31
  9.5 1.0 %multiply_bitcast_fusion = f32[16,8,512]{2,1,0:T(8,128)S(1)} fusion(f32[1,16,8,512]{3,2,1,0:T(8,128)} %param.8, f32[16,512]{1,0:T(8,128)S(1)} %multiply_bitcast_fusion.1), kind=kLoop, calls=%fused_computation.12 | loop fusion | flops 65536 | bytes 557056 | tf_op jit(solution)/shard_map/squeeze | solution.py:45
  10.5 0.0 copy-start.4
  10.5 0.0 copy-start.1
  10.6 0.0 copy-start.2
  10.6 0.4 %fusion.6 = f32[16,8,512]{2,0,1:T(8,128)S(1)} fusion(f32[16,8,512]{2,1,0:T(8,128)S(1)} %multiply_bitcast_fusion, s32[16]{0:T(128)S(1)} %fusion.21), kind=kOutput, calls=%fused_computation.8 | convolution fusion | flops 12583168 | bytes 524352 | tf_op jit(solution)/shard_map/qs,sfc->qfc/dot_general | solution.py:45
  11.0 0.2 copy-done.4
  11.2 0.1 copy-done.1
  11.3 0.0 copy-done.2
  11.3 0.6 %convert_reduce_fusion.1 = (s32[]{:T(128)}, f32[64,128]{1,0:T(8,128)S(1)}) fusion(f32[64,128]{1,0:T(8,128)S(1)} %copy-done.1, s32[64,128]{1,0:T(8,128)S(1)} %copy-done.2), kind=kLoop, calls=%fused_computation.13 | loop fusion | flops 40959 | bytes 98308 | tf_op jit(solution)/shard_map/reduce_sum | solution.py:11
  12.0 0.9 %copy.14 = f32[16,8,512]{2,1,0:T(8,128)} copy(f32[16,8,512]{2,0,1:T(8,128)S(1)} %fusion.6) | data formatting | bytes 524288 | tf_op jit(solution)/shard_map/qs,sfc->qfc/dot_general | solution.py:45
  12.8 1.4 %all-to-all-done = f32[4,4,1]{1,2,0:T(1,128)S(1)} async-done(((f32[4,4,1]{1,2,0:T(1,128)}), f32[4,4,1]{1,2,0:T(1,128)S(1)}, u32[]{:S(2)}, u32[]{:S(2)}) %all-to-all-start) | async-done | bytes 96 | tf_op jit(solution)/shard_map/all_to_all | solution.py:52
  14.2 3.9 %all-to-all-start.1 = ((f32[16,8,512]{2,1,0:T(8,128)}), f32[16,8,512]{2,1,0:T(8,128)S(1)}, u32[]{:S(2)}, u32[]{:S(2)}) async-start(f32[16,8,512]{2,1,0:T(8,128)} %copy.14), calls=%async_computation.1 | async-start | bytes 524288 | tf_op jit(solution)/shard_map/all_to_all | solution.py:51
  21.3 0.2 convert_reduce_fusion
  21.5 0.5 %broadcast.161 = f32[]{:T(128)} broadcast(f32[]{:T(128)} %constant.126), dimensions={} | broadcast | bytes 8 | tf_op jit(solution)/shard_map/all_to_all | solution.py:52
  22.0 0.7 %reduce.4 = f32[4,4]{1,0:T(4,128)S(1)} reduce(f32[4,4,1]{1,2,0:T(1,128)S(1)} %all-to-all-done, f32[]{:T(128)} %broadcast.161), dimensions={2}, to_apply=%all_to_all.10.reduce_sub_computation.3 | reduce | bytes 132 | tf_op jit(solution)/shard_map/all_to_all | solution.py:52
  22.7 0.1 eq.52
  22.8 3.6 %all-to-all-done.1 = f32[16,8,512]{2,1,0:T(8,128)S(1)} async-done(((f32[16,8,512]{2,1,0:T(8,128)}), f32[16,8,512]{2,1,0:T(8,128)S(1)}, u32[]{:S(2)}, u32[]{:S(2)}) %all-to-all-start.1) | async-done | bytes 262176 | tf_op jit(solution)/shard_map/all_to_all | solution.py:51
  26.4 0.4 %fusion.4 = f32[16,8,512]{2,0,1:T(8,128)S(1)} fusion(f32[16,8,512]{2,1,0:T(8,128)S(1)} %all-to-all-done.1, f32[16]{0:T(128)S(1)} %eq.52, f32[16]{0:T(128)S(1)} %iota_convert_fusion), kind=kOutput, calls=%fused_computation.6 | convolution fusion | flops 12583168 | bytes 524416 | tf_op jit(solution)/shard_map/nw,whl->nhl/dot_general | solution.py:57
  26.8 0.1 reshape.55
  26.9 0.3 fusion.3
  27.2 6.4 %all-reduce = (s32[8]{0:T(128)S(1)}, s32[8]{0:T(128)S(1)}, s32[]{:T(128)}, s32[]{:T(128)}, s32[8]{0:T(128)S(1)}, /*index=5*/s32[8]{0:T(128)S(1)}) all-reduce(s32[8]{0:T(128)S(1)} %get-tuple-element.16, s32[8]{0:T(128)S(1)} %get-tuple-element.17, s32[]{:T(128)S(6)} %select_n.37, ...), channel_id=1, replica_groups=mesh['member'=4,'lat'=2,'lon'=4] {'lon'}, use_global_device_ids=true, to_apply=%region_9.10 | all-reduce | flops 34 | bytes 272 | tf_op jit(solution)/shard_map/psum | solution.py:68
  33.6 2.5 %all-reduce.1 = (s32[8]{0:T(128)S(1)}, s32[8]{0:T(128)S(1)}, s32[]{:T(128)}, s32[]{:T(128)}, s32[8]{0:T(128)S(1)}, /*index=5*/s32[8]{0:T(128)S(1)}) all-reduce(s32[8]{0:T(128)S(1)} %get-tuple-element.2, s32[8]{0:T(128)S(1)} %get-tuple-element.3, s32[]{:T(128)} %get-tuple-element.4, ...), channel_id=1, replica_groups=mesh['member'=4,'lat'=2,'lon'=4] {'lat'}, use_global_device_ids=true, to_apply=%region_10.11 | all-reduce | flops 34 | bytes 272 | tf_op jit(solution)/shard_map/psum | solution.py:67
  37.3 0.5 %fusion.28 = (f32[8]{0:T(128)}, f32[8]{0:T(128)S(1)}) fusion(s32[8]{0:T(128)S(1)} %copy-done.4, s32[8]{0:T(128)S(1)} %get-tuple-element.12, s32[8]{0:T(128)S(1)} %get-tuple-element.13, f32[]{:T(128)S(6)} %div.93, s32[8]{0:T(128)S(1)} %get-tuple-element.8, s32[8]{0:T(128)S(1)} %get-tuple-element.9), kind=kLoop, calls=%fused_computation.61 | loop fusion | flops 120 | bytes 228 | tf_op jit(solution)/shard_map/mul | solution.py:81
  37.9 0.8 %add_multiply_fusion = f32[8,64,128]{2,1,0:T(8,128)} fusion(f32[8,64,128]{2,1,0:T(8,128)S(1)} %bitcast.56, f32[8]{0:T(128)S(1)} %get-tuple-element.21, f32[64,128]{1,0:T(8,128)S(1)} %copy-done.1, f32[8]{0:T(128)S(1)} %shift-left_convert_fusion, f32[64,128]{1,0:T(8,128)S(1)} %get-tuple-element.19), kind=kLoop, calls=%fused_computation.10 | loop fusion | flops 262144 | bytes 589888 | tf_op jit(solution)/shard_map/mul | solution.py:79
  (10 shorter events, 0.1 us)
Async XLA Ops:
  0.6 0.7 %copy-start.5 = (s32[1,16]{1,0:T(1,128)S(1)}, s32[1,16]{1,0:T(1,128)}, u32[]{:S(2)}) copy-start(s32[1,16]{1,0:T(1,128)} %param.12) | copy-start | bytes 196
  0.6 8.1 %copy-start.3 = (s32[1,16,512]{2,1,0:T(8,128)S(1)}, s32[1,16,512]{2,1,0:T(8,128)}, u32[]{:S(2)}) copy-start(s32[1,16,512]{2,1,0:T(8,128)} %param.10) | copy-start | bytes 98308
  2.4 11.8 %all-to-all-start = ((f32[4,4,1]{1,2,0:T(1,128)}), f32[4,4,1]{1,2,0:T(1,128)S(1)}, u32[]{:S(2)}, u32[]{:S(2)}) async-start(f32[4,4,1]{1,2,0:T(1,128)} %bitcast.6), calls=%async_computation | async-start | bytes 4096 | tf_op jit(solution)/shard_map/all_to_all | solution.py:52
  10.5 0.7 %copy-start.4 = (s32[8]{0:T(128)S(1)}, s32[8]{0:T(128)}, u32[]{:S(2)}) copy-start(s32[8]{0:T(128)} %param.15) | copy-start | bytes 100
  10.5 0.8 %copy-start.1 = (f32[64,128]{1,0:T(8,128)S(1)}, f32[64,128]{1,0:T(8,128)}, u32[]{:S(2)}) copy-start(f32[64,128]{1,0:T(8,128)} %param.13) | copy-start | bytes 98308
  10.6 0.8 %copy-start.2 = (s32[64,128]{1,0:T(8,128)S(1)}, s32[64,128]{1,0:T(8,128)}, u32[]{:S(2)}) copy-start(s32[64,128]{1,0:T(8,128)} %param.14) | copy-start | bytes 98308
  12.8 8.5 %copy-start = (f32[1,16,8,512]{3,2,1,0:T(8,128)S(1)}, f32[1,16,8,512]{3,2,1,0:T(8,128)}, u32[]{:S(2)}) copy-start(f32[1,16,8,512]{3,2,1,0:T(8,128)} %param.8) | copy-start | bytes 786436
  14.2 12.2 %all-to-all-start.1 = ((f32[16,8,512]{2,1,0:T(8,128)}), f32[16,8,512]{2,1,0:T(8,128)S(1)}, u32[]{:S(2)}, u32[]{:S(2)}) async-start(f32[16,8,512]{2,1,0:T(8,128)} %copy.14), calls=%async_computation.1 | async-start | bytes 524288 | tf_op jit(solution)/shard_map/all_to_all | solution.py:51
